TPU v7x, 32 devices: a whole 2x2x4 slice. The times are simulated.
32 devices in a mesh: wide: 8 (over z, x), narrow: 4 (over y, core).
Axes of the slice: x: 2, y: 2, z: 4, core: 2. Of those that a mesh axis runs over, the one named last changes fastest.
Arguments:
- tokens: bfloat16 [24, 4, 256, 768], P('wide', 'narrow'), may hold values from -6 to 6
- condition: bfloat16 [24, 768], P('wide'), may hold values from -6 to 6
- counts: int32 [8], P('wide'), may hold values from 1 to 3, as said below
- w_mod: bfloat16 [768, 4608], replicated, may hold values from -0.21875 to 0.21875
- w_qkv: bfloat16 [768, 2304], replicated, may hold values from -0.21875 to 0.21875
- w_out: bfloat16 [768, 768], replicated, may hold values from -1.75 to 1.75
- w_up: bfloat16 [768, 3072], replicated, may hold values from -0.21875 to 0.21875
- w_down: bfloat16 [3072, 768], replicated, may hold values from -0.109375 to 0.109375
- conv_attn: bfloat16 [768, 9], replicated, may hold values from -2 to 2
- conv_ffn: bfloat16 [3072, 9], replicated, may hold values from -2 to 2
- cotangent: bfloat16 [24, 4, 256, 768], P('wide', 'narrow'), may hold values from -6 to 6
Outputs:
- output: bfloat16 [24, 4, 256, 768], P('wide', 'narrow')
- token_grad: bfloat16 [24, 4, 256, 768], P('wide', 'narrow')
- cond_grad: float32 [24, 768], P('wide')
- mod_grad: float32 [768, 4608], P(('wide', 'narrow'))
- qkv_grad: float32 [768, 2304], P(('wide', 'narrow'))
- proj_grad: float32 [768, 768], P(('wide', 'narrow'))
- up_grad: float32 [768, 3072], P(('wide', 'narrow'))
- down_grad: float32 [3072, 768], P(('wide', 'narrow'))
- conv_attn_grad: float32 [768, 9], P(('wide', 'narrow'))
- conv_ffn_grad: float32 [3072, 9], P(('wide', 'narrow'))
Inputs may be any that keep to these rules, and one draw needn't show every extreme that they name: `counts`: items with index b mod 3 at or above the count of their index of wide are padding; some index of wide holds 3 live items.
All inputs are finite; a program needn't handle non-finite values.
Results may differ from a plain program's by a relative error of at most 0.017.
The roundings to bfloat16 on the way count: a program that leaves them out, or rounds other values in their place, can miss the bound.
Values may be sent and summed in bfloat16 or wider, within the bound.
A program may use at most 192 MiB of HBM per device.

v0:
```python
import math
import jax
import jax.numpy as jnp
from jax import lax
from jax.sharding import PartitionSpec as P

HEADS = 12
HEAD_DIM = 64
epsilon = 1e-06


def from_partner(shard, axis, bit):
    return lax.ppermute(shard, axis, [(i, i ^ 1 << bit) for i in range(lax.axis_size(axis))])


def normed(field_map):
    average = jnp.mean(field_map, -1, keepdims=True)
    centred = field_map - average
    variance = jnp.mean(centred * centred, -1, keepdims=True)
    return centred * lax.rsqrt(variance + epsilon)


def modulate(field_map, shift, scale):
    return normed(field_map) * (1.0 + scale) + shift


def gelu_tanh(field_map):
    return jax.nn.gelu(field_map, approximate=True)


def attn_across(outgoing):
    return from_partner(outgoing, "narrow", 0)


def attn_down(outgoing):
    return from_partner(outgoing, "narrow", 1)


def ffn_across(outgoing):
    return from_partner(outgoing, "narrow", 0)


def ffn_down(outgoing):
    return from_partner(outgoing, "narrow", 1)


def extend(field_map, row_half, col_half, across, down):
    outgoing = jnp.where(col_half == 0, field_map[:, :, -1:], field_map[:, :, :1])
    incoming = across(outgoing)
    zeros_rim = jnp.zeros_like(incoming)
    left_rim = jnp.where(col_half == 1, incoming, zeros_rim)
    right_rim = jnp.where(col_half == 0, incoming, zeros_rim)
    widened = jnp.concatenate([left_rim, field_map, right_rim], 2)
    outgoing = jnp.where(row_half == 0, widened[:, -1:], widened[:, :1])
    incoming = down(outgoing)
    zeros_rim = jnp.zeros_like(incoming)
    top_rim = jnp.where(row_half == 1, incoming, zeros_rim)
    bottom_rim = jnp.where(row_half == 0, incoming, zeros_rim)
    return jnp.concatenate([top_rim, widened, bottom_rim], 1)


def apply_taps(padded, kernel, side_len, flipped):
    summed = jnp.zeros((padded.shape[0], side_len, side_len, padded.shape[3]), jnp.float32)
    weights_f = kernel.astype(jnp.float32)
    for stencil in range(9):
        row_off = stencil // 3
        col_off = stencil % 3
        if flipped:
            row_off = 2 - row_off
            col_off = 2 - col_off
        window = padded[:, row_off : row_off + side_len, col_off : col_off + side_len].astype(
            jnp.float32
        )
        summed = summed + window * weights_f[:, stencil]
    return summed


def tap_grads(padded, grad_map, side_len):
    grad_f = grad_map.astype(jnp.float32)
    columns = []
    for stencil in range(9):
        row_off = stencil // 3
        col_off = stencil % 3
        window = padded[:, row_off : row_off + side_len, col_off : col_off + side_len].astype(
            jnp.float32
        )
        columns.append(jnp.sum(window * grad_f, axis=(0, 1, 2)))
    return jnp.stack(columns, 1)


def to_groups(field_map):
    count, side_len, _, channels = field_map.shape
    quarter = side_len // 2
    pieces = field_map.reshape(count, quarter, 2, quarter, 2, channels).transpose(0, 2, 4, 1, 3, 5)
    pieces = pieces.reshape(count, 4, quarter * quarter, channels)
    incoming = lax.all_to_all(pieces, "narrow", split_axis=1, concat_axis=1, tiled=True)
    return incoming.reshape(count, 4 * quarter * quarter, channels)


def to_quads(group_rows):
    count, rows_all, channels = group_rows.shape
    pieces = group_rows.reshape(count, 4, rows_all // 4, channels)
    incoming = lax.all_to_all(pieces, "narrow", split_axis=1, concat_axis=1, tiled=True)
    quarter = math.isqrt(rows_all // 4)
    incoming = incoming.reshape(count, 2, 2, quarter, quarter, channels).transpose(0, 3, 1, 4, 2, 5)
    return incoming.reshape(count, 2 * quarter, 2 * quarter, channels)


def split_heads(groups, w_qkv):
    count, rows_all, _ = groups.shape
    triple = jnp.dot(groups, w_qkv, preferred_element_type=jnp.float32).astype(jnp.bfloat16)
    triple = triple.reshape(count, rows_all, 3, HEADS, HEAD_DIM)
    return (triple[:, :, 0], triple[:, :, 1], triple[:, :, 2])


def score(queries, key_rows):
    return jnp.einsum(
        "iqhe,ikhe->ihqk", queries, key_rows, preferred_element_type=jnp.float32
    ) * HEAD_DIM ** (-0.5)


def narrow_sum(part):
    for bit in range(lax.axis_size("narrow").bit_length() - 1):
        part = part + from_partner(part, "narrow", bit)
    return part


def wide_gather(block):
    count = lax.axis_size("wide")
    place = lax.axis_index("wide")
    held = block[None]
    for bit in range(count.bit_length() - 1):
        other = from_partner(held, "wide", bit)
        mine_high = place >> bit & 1
        low = jnp.where(mine_high == 1, other, held)
        high = jnp.where(mine_high == 1, held, other)
        held = jnp.concatenate([low, high], 0)
    return held.reshape((count * block.shape[0],) + block.shape[1:])


def split_dot(exact, coarse, dims):
    high = exact.astype(jnp.bfloat16)
    low = (exact - high.astype(jnp.float32)).astype(jnp.bfloat16)
    high_dot = lax.dot_general(high, coarse, (dims, ((), ())), preferred_element_type=jnp.float32)
    low_dot = lax.dot_general(low, coarse, (dims, ((), ())), preferred_element_type=jnp.float32)
    return high_dot + low_dot


def halving_sum(blocks, colour):
    wide_bits = lax.axis_size("wide").bit_length() - 1
    narrow_bits = lax.axis_size("narrow").bit_length() - 1
    order = [("narrow", 0)]
    first = [("wide", 0), ("narrow", 1)]
    order += first if colour == 0 else first[::-1]
    order += [("wide", bit) for bit in range(1, wide_bits)]
    names = [("wide", bit) for bit in range(wide_bits - 1, -1, -1)]
    names += [("narrow", bit) for bit in range(narrow_bits - 1, -1, -1)]
    held = blocks.reshape((2,) * len(names) + blocks.shape[1:])
    for step, (axis, bit) in enumerate(order):
        where = names.index((axis, bit))
        names.pop(where)
        mine = lax.axis_index(axis) >> bit & 1
        keep = lax.dynamic_index_in_dim(held, mine, where, keepdims=False)
        give = lax.dynamic_index_in_dim(held, 1 - mine, where, keepdims=False)
        got = from_partner(give, axis, bit)
        held = keep.astype(jnp.float32) + got.astype(jnp.float32)
        if step < len(order) - 1:
            held = held.astype(jnp.bfloat16)
    return held


def shards(
    tokens, condition, counts, w_mod, w_qkv, w_out, w_up, w_down, conv_attn, conv_ffn, cotangent
):
    item_count, _, quad_rows, channels = tokens.shape
    half_side = math.isqrt(quad_rows)
    corner = lax.axis_index("narrow")
    row_half = corner // 2
    col_half = corner % 2
    living = (jnp.arange(item_count, dtype=jnp.int32) < counts[0]).astype(jnp.float32)[
        :, None, None, None
    ]
    start_map = tokens.reshape(item_count, half_side, half_side, channels).astype(jnp.float32)
    cond_f = condition.astype(jnp.float32)
    lifted = jax.nn.silu(cond_f).astype(jnp.bfloat16)
    all_lifted = wide_gather(lifted)
    modulation = jnp.dot(lifted, w_mod, preferred_element_type=jnp.float32).reshape(
        item_count, 6, channels
    )
    pieces = [modulation[:, place][:, None, None, :] for place in range(6)]
    shift_a, scale_a, gate_a, shift_f, scale_f, gate_f = pieces
    first_f, pull_attn_norm = jax.vjp(modulate, start_map, shift_a, scale_a)
    first_in = first_f.astype(jnp.bfloat16)
    padded_attn = extend(first_in, row_half, col_half, attn_across, attn_down)
    mixed_map = apply_taps(padded_attn, conv_attn, half_side, False).astype(jnp.bfloat16)
    groups = to_groups(mixed_map)
    queries, key_rows, values = split_heads(groups, w_qkv)
    scores = score(queries, key_rows)
    peak = jnp.max(scores, -1, keepdims=True)
    raised_exp = jnp.exp(scores - peak)
    summed = jnp.sum(raised_exp, -1, keepdims=True)
    attn_probs = (raised_exp / summed).astype(jnp.bfloat16)
    log_total = peak + jnp.log(summed)
    attended = jnp.einsum("ihqk,ikhe->iqhe", attn_probs, values, preferred_element_type=jnp.float32)
    attended = attended.astype(jnp.bfloat16).reshape(item_count, quad_rows, channels)
    returned = to_quads(attended)
    branch = jnp.dot(returned, w_out, preferred_element_type=jnp.float32)
    hidden_one = start_map + gate_a * branch
    second_f, pull_ffn_norm = jax.vjp(modulate, hidden_one, shift_f, scale_f)
    second = second_f.astype(jnp.bfloat16)
    raised = jnp.dot(second, w_up, preferred_element_type=jnp.float32).astype(jnp.bfloat16)
    padded_ffn = extend(raised, row_half, col_half, ffn_across, ffn_down)
    filtered = apply_taps(padded_ffn, conv_ffn, half_side, False)
    activated = gelu_tanh(filtered).astype(jnp.bfloat16)
    branch_two = jnp.dot(activated, w_down, preferred_element_type=jnp.float32)
    output = ((hidden_one + gate_f * branch_two) * living).astype(jnp.bfloat16)
    grad_res = (
        cotangent.reshape(item_count, half_side, half_side, channels).astype(jnp.float32) * living
    )
    d_gate_f = jnp.sum(grad_res * branch_two, (1, 2))
    d_branch_two = (grad_res * gate_f).astype(jnp.bfloat16)
    down_grad = jnp.einsum(
        "ixyf,ixyd->fd", activated, d_branch_two, preferred_element_type=jnp.float32
    )
    d_activated = jnp.einsum(
        "ixyd,fd->ixyf", d_branch_two, w_down, preferred_element_type=jnp.float32
    )
    again = jnp.dot(second, w_up, preferred_element_type=jnp.float32).astype(jnp.bfloat16)
    kept_pad = extend(again, row_half, col_half, ffn_across, ffn_down)
    kept_filter = apply_taps(kept_pad, conv_ffn, half_side, False)
    _, gelu_pull = jax.vjp(gelu_tanh, kept_filter)
    d_filtered = gelu_pull(d_activated)[0].astype(jnp.bfloat16)
    conv_ffn_grad = tap_grads(kept_pad, d_filtered, half_side)
    d_padded_ffn = extend(d_filtered, row_half, col_half, ffn_across, ffn_down)
    d_raised = apply_taps(d_padded_ffn, conv_ffn, half_side, True).astype(jnp.bfloat16)
    up_grad = jnp.einsum("ixyd,ixyf->df", second, d_raised, preferred_element_type=jnp.float32)
    d_second = jnp.einsum("ixyf,df->ixyd", d_raised, w_up, preferred_element_type=jnp.float32)
    d_hidden_part, d_shift_f, d_scale_f = pull_ffn_norm(d_second)
    d_hidden = grad_res + d_hidden_part
    d_gate_a = jnp.sum(d_hidden * branch, (1, 2))
    d_branch = (d_hidden * gate_a).astype(jnp.bfloat16)
    proj_grad = jnp.einsum("ixyd,ixye->de", returned, d_branch, preferred_element_type=jnp.float32)
    d_returned = jnp.einsum(
        "ixye,de->ixyd", d_branch, w_out, preferred_element_type=jnp.float32
    ).astype(jnp.bfloat16)
    d_attended = to_groups(d_returned).reshape(item_count, quad_rows, HEADS, HEAD_DIM)
    queries, key_rows, values = split_heads(groups, w_qkv)
    scores = score(queries, key_rows)
    exact = jnp.exp(scores - log_total)
    rounded = exact.astype(jnp.bfloat16)
    d_probs = jnp.einsum("iqhe,ikhe->ihqk", d_attended, values, preferred_element_type=jnp.float32)
    d_values = jnp.einsum(
        "ihqk,iqhe->ikhe", rounded, d_attended, preferred_element_type=jnp.float32
    )
    d_scores = (exact * (d_probs - jnp.sum(d_probs * exact, -1, keepdims=True))).astype(
        jnp.bfloat16
    )
    d_queries = jnp.einsum(
        "ihqk,ikhe->iqhe", d_scores, key_rows, preferred_element_type=jnp.float32
    ) * HEAD_DIM ** (-0.5)
    d_keys = jnp.einsum(
        "ihqk,iqhe->ikhe", d_scores, queries, preferred_element_type=jnp.float32
    ) * HEAD_DIM ** (-0.5)
    d_triple = (
        jnp.stack([d_queries, d_keys, d_values], 2)
        .astype(jnp.bfloat16)
        .reshape(item_count, quad_rows, 3 * channels)
    )
    qkv_grad = jnp.einsum("iqd,iqe->de", groups, d_triple, preferred_element_type=jnp.float32)
    d_groups = jnp.einsum(
        "iqe,de->iqd", d_triple, w_qkv, preferred_element_type=jnp.float32
    ).astype(jnp.bfloat16)
    d_mixed = to_quads(d_groups)
    conv_attn_grad = tap_grads(padded_attn, d_mixed, half_side)
    d_padded_attn = extend(d_mixed, row_half, col_half, attn_across, attn_down)
    d_first = apply_taps(d_padded_attn, conv_attn, half_side, True).astype(jnp.bfloat16)
    d_start, d_shift_a, d_scale_a = pull_attn_norm(d_first.astype(jnp.float32))
    token_grad = (d_hidden + d_start).astype(jnp.bfloat16).reshape(tokens.shape)
    flat_parts = [
        d_shift_a.reshape(item_count, channels),
        d_scale_a.reshape(item_count, channels),
        d_gate_a,
        d_shift_f.reshape(item_count, channels),
        d_scale_f.reshape(item_count, channels),
        d_gate_f,
    ]
    d_modulation = jnp.stack(flat_parts, 1).reshape(item_count, 6 * channels)
    d_modulation = narrow_sum(d_modulation)
    _, silu_pull = jax.vjp(jax.nn.silu, cond_f)
    d_lifted = split_dot(d_modulation, w_mod, ((1,), (1,)))
    cond_grad = silu_pull(d_lifted)[0]
    all_modulation = wide_gather(d_modulation)
    block_rows = channels // (lax.axis_size("wide") * lax.axis_size("narrow"))
    own_block = lax.axis_index("wide") * lax.axis_size("narrow") + corner
    own_lifted = lax.dynamic_slice_in_dim(all_lifted, own_block * block_rows, block_rows, 1)
    mod_sum = split_dot(all_modulation, own_lifted, ((0,), (0,))).T
    blocks = lax.axis_size("wide") * lax.axis_size("narrow")
    up_blocks = up_grad.astype(jnp.bfloat16).reshape(blocks, -1, up_grad.shape[1])
    down_blocks = down_grad.astype(jnp.bfloat16).reshape(blocks, -1, channels)
    up_sum = halving_sum(up_blocks, 0)
    down_sum = halving_sum(down_blocks, 1)
    qkv_blocks = qkv_grad.astype(jnp.bfloat16).reshape(blocks, -1, 3 * channels)
    proj_blocks = proj_grad.astype(jnp.bfloat16).reshape(blocks, -1, channels)
    taps = jnp.concatenate(
        [conv_attn_grad.reshape(blocks, -1), conv_ffn_grad.reshape(blocks, -1)], 1
    )
    rows = qkv_blocks.shape[1]
    taps_len = taps.shape[1]
    taps_wide = -(-taps_len // (rows * 128)) * 128
    taps = jnp.pad(taps, ((0, 0), (0, rows * taps_wide - taps_len)))
    taps = taps.astype(jnp.bfloat16).reshape(blocks, rows, taps_wide)
    left_sum = halving_sum(qkv_blocks[:, :, : 2 * channels], 0)
    right = jnp.concatenate([qkv_blocks[:, :, 2 * channels :], proj_blocks, taps], 2)
    right_sum = halving_sum(right, 1)
    qkv_sum = jnp.concatenate([left_sum, right_sum[:, :channels]], 1)
    proj_sum = right_sum[:, channels : 2 * channels]
    tap_sums = right_sum[:, 2 * channels :].reshape(-1)
    attn_len = conv_attn_grad.size // blocks
    conv_attn_sum = tap_sums[:attn_len].reshape(-1, 9)
    conv_ffn_sum = tap_sums[attn_len:taps_len].reshape(-1, 9)
    return (
        output.reshape(tokens.shape),
        token_grad,
        cond_grad,
        mod_sum,
        qkv_sum,
        proj_sum,
        up_sum,
        down_sum,
        conv_attn_sum,
        conv_ffn_sum,
    )


def solution(mesh):
    in_specs = (
        P("wide", "narrow", None, None),
        P("wide", None),
        P("wide"),
        P(),
        P(),
        P(),
        P(),
        P(),
        P(),
        P(),
        P("wide", "narrow", None, None),
    )
    out_specs = (
        P("wide", "narrow", None, None),
        P("wide", "narrow", None, None),
        P("wide", None),
        P(("wide", "narrow"), None),
        P(("wide", "narrow"), None),
        P(("wide", "narrow"), None),
        P(("wide", "narrow"), None),
        P(("wide", "narrow"), None),
        P(("wide", "narrow"), None),
        P(("wide", "narrow"), None),
    )
    return jax.shard_map(shards, mesh=mesh, in_specs=in_specs, out_specs=out_specs, check_vma=False)
```

profile of v0, /device:TPU:0, one launch (start us, length us, event | category | flops | bytes accessed | tf_op | source)
XLA Modules:
  0.0 598.8 jit_solution(1541009015088107314)
XLA Ops:
  5.1 4.7 fusion.146
  47.6 4.6 all-to-all-start
  55.2 12.9 %all-to-all-done = bf16[3,4,64,768]{3,2,0,1:T(8,128)(2,1)} async-done(((bf16[3,4,64,768]{3,2,0,1:T(8,128)(2,1)}), bf16[3,4,64,768]{3,2,0,1:T(8,128)(2,1)}, u32[]{:S(2)}, u32[]{:S(2)}) %all-to-all-start) | async-done | bytes 1179680 | tf_op jit(solution)/shard_map/all_to_all | solution.py:96
  74.8 5.8 copy.105
  87.9 4.6 fusion.94
  92.5 4.6 reshape_reshape.12
  97.1 5.1 copy.110
  102.2 4.8 all-to-all-start.1
  114.7 8.1 %all-to-all-done.1 = bf16[3,4,64,768]{3,2,0,1:T(8,128)(2,1)} async-done(((bf16[3,4,64,768]{3,2,0,1:T(8,128)(2,1)}), bf16[3,4,64,768]{3,2,0,1:T(8,128)(2,1)}, u32[]{:S(2)}, u32[]{:S(2)}) %all-to-all-start.1) | async-done | bytes 1179680 | tf_op jit(solution)/shard_map/all_to_all | solution.py:103
  130.1 5.0 fusion.142
  149.9 10.7 %collective-permute-done.3 = bf16[3,1,18,3072]{3,2,1,0:T(8,128)(2,1)} collective-permute-done((bf16[3,1,18,3072]{3,2,1,0:T(8,128)(2,1)}, bf16[3,1,18,3072]{3,2,1,0:T(8,128)(2,1)}, u32[]{:S(2)}, u32[]{:S(2)}) %collective-permute-start.3) | collective-permute-done | bytes 331808 | tf_op jit(solution)/shard_map/ppermute | solution.py:13
  161.8 12.1 %maximum_maximum_fusion = (bf16[3,17,18,3072]{3,2,1,0:T(8,128)(2,1)S(1)}, bf16[3,17,18,3072]{3,2,1,0:T(8,128)(2,1)S(1)}) fusion(bf16[3,16,1,3072]{3,2,1,0:T(2,128)(2,1)} %copy-done.27, bf16[3,16,16,3072]{3,2,1,0:T(8,128)(2,1)} %copy-done.5, bf16[3,16,1,3072]{3,2,1,0:T(2,128)(2,1)} %copy-done.25, bf16[3,1,18,3072]{3,2,1,0:T(8,128)(2,1)S(1)} %get-tuple-element.121, ...), kind=kLoop, calls=%fused_computation.61 | loop fusion | flops 45121536 | bytes 17252352 | tf_op jit(solution)/shard_map/concatenate | solution.py:59
  174.1 15.6 %fusion.7 = f32[3,16,16,3072]{3,2,1,0:T(8,128)} fusion(bf16[3,16,16,3072]{3,2,1,0:T(8,128)(2,1)S(1)} %bitcast.307, bf16[3,16,1,3072]{3,2,1,0:T(2,128)(2,1)} %copy-done.27, bf16[3,16,1,3072]{3,2,1,0:T(2,128)(2,1)S(1)} %copy-done.26, f32[3072]{0:T(1024)S(1)} %bitcast.354, f32[3072]{0:T(1024)S(1)} %bitcast.352, f32[3072]{0:T(1024)S(1)} %bitcast.350, ...), kind=kLoop, calls=%fused_computation.28 | loop fusion | flops 75497472 | bytes 43167744 | tf_op jit(solution)/shard_map/add | solution.py:74
  189.7 35.1 %fusion.29 = (bf16[3072]{0:T(1024)(128)(2,1)}, bf16[3072]{0:T(1024)(128)(2,1)}, bf16[3072]{0:T(1024)(128)(2,1)}, bf16[3072]{0:T(1024)(128)(2,1)}, bf16[3072]{0:T...) fusion(bf16[3,17,18,3072]{3,2,1,0:T(8,128)(2,1)} %copy-done.4, ...), kind=kOutput, calls=%fused_computation.50 | convolution fusion | flops 3753612288 | bytes 53738508 | tf_op jit(solution)/shard_map/ixyd,fd->ixyf/dot_general | solution.py:225
  237.7 9.7 %bitcast_convert_fusion = bf16[3072,768]{1,0:T(8,128)(2,1)} fusion(bf16[3,16,16,768]{3,2,1,0:T(8,128)(2,1)S(1)} %bitcast.359, f32[3]{0:T(128)S(1)} %compare_convert_fusion, f32[3,768]{1,0:T(4,128)S(1)} %copy-done.112, f32[3,16,16,3072]{3,2,1,0:T(8,128)} %fusion.7), kind=kOutput, calls=%fused_computation.51 | convolution fusion | flops 3649830912 | bytes 15344652 | tf_op jit(solution)/shard_map/ixyf,ixyd->fd/dot_general | solution.py:222
  267.8 10.0 %pad_maximum_fusion.1 = (bf16[3,17,18,3072]{3,2,1,0:T(8,128)(2,1)S(1)}, bf16[3,17,18,3072]{3,2,1,0:T(8,128)(2,1)S(1)}) fusion(bf16[3,1,18,3072]{3,2,1,0:T(8,128)(2,1)S(1)} %get-tuple-element.119, bf16[3,16,1,3072]{3,2,1,0:T(2,128)(2,1)S(1)} %copy-done.31, bf16[3,16,16,3072]{3,2,1,0:T(8,128)(2,1)S(1)} %bitcast.305, ...), kind=kLoop, calls=%fused_computation.63 | loop fusion | flops 45121536 | bytes 17252352 | tf_op jit(solution)/shard_map/concatenate | solution.py:59
  278.0 15.8 %fusion.20 = bf16[3,16,16,3072]{3,2,1,0:T(8,128)(2,1)} fusion(bf16[3,16,16,3072]{3,2,1,0:T(8,128)(2,1)S(1)} %bitcast.305, bf16[3,17,18,3072]{3,2,1,0:T(8,128)(2,1)S(1)} %get-tuple-element.100, bf16[3,16,1,3072]{3,2,1,0:T(2,128)(2,1)S(1)} %copy-done.29, bf16[3,16,1,3072]{3,2,1,0:T(2,128)(2,1)} %copy-done.30, ...), kind=kLoop, calls=%fused_computation.41 | loop fusion | flops 77856768 | bytes 38449152 | tf_op jit(solution)/shard_map/convert_element_type | solution.py:235
  293.9 8.6 %multiply_reduce_fusion.5 = (f32[3,16,16]{2,1,0:T(8,128)S(1)}, f32[3,16,16,768]{3,2,1,0:T(8,128)S(1)}) fusion(f32[3,16,16,768]{3,2,1,0:T(8,128)} %copy-done.12, f32[3,768]{1,0:T(4,128)S(1)} %copy-done.93, f32[3,16,16]{2,1,0:T(8,128)S(1)} %copy-done.53, bf16[3,16,16,3072]{3,2,1,0:T(8,128)(2,1)} %fusion.20, bf16[768,3072]{1,0:T(8,128)(2,1)} %param.17), kind=kOutput, calls=%fused_computation.170 | convolution fusion | flops 3626237184 | bytes 14171136 | tf_op jit(solution)/shard_map/ixyf,df->ixyd/dot_general | solution.py:237
  302.6 6.4 %bitcast_convert_fusion.1 = bf16[768,3072]{1,0:T(8,128)(2,1)} fusion(bf16[3,16,16,3072]{3,2,1,0:T(8,128)(2,1)S(1)} %copy-done.33, f32[3,16,16,768]{3,2,1,0:T(8,128)S(1)} %copy-done.13, f32[3,768]{1,0:T(4,128)S(1)} %copy-done.115, f32[3,768]{1,0:T(4,128)S(1)} %copy-done.93, f32[3,16,16]{2,1,0:T(8,128)S(1)} %copy-done.81, f32[3,16,16]{2,1,0:T(8,128)S(1)} %copy-done.53), kind=kOutput, calls=%fused_computation.52 | convolution fusion | flops 3629187072 | bytes 11821056 | tf_op jit(solution)/shard_map/ixyd,ixyf->df/dot_general | solution.py:236
  311.5 10.4 %fusion.86 = (f32[3,768]{1,0:T(4,128)}, bf16[3,16,16,768]{3,2,1,0:T(8,128)(2,1)}, f32[3,768]{1,0:T(4,128)}, f32[3,16,16,768]{3,2,1,0:T(8,128)S(1)}) fusion(bf16[3,16,16,768]{3,2,1,0:T(8,128)(2,1)S(1)} %bitcast.360, f32[3]{0:T(128)S(1)} %compare_convert_fusion, f32[3,16,16,768]{3,2,1,0:T(8,128)S(1)} %copy-done.13, f32[3,768]{1,0:T(4,128)S(1)} %copy-done.113, ...), kind=kOutput, calls=%fused_computation.159 | convolution fusion | flops 3655724544 | bytes 26001420 | tf_op jit(solution)/shard_map/dot_general | solution.py:215
  352.0 5.2 copy.121
  361.7 6.8 %fusion.87 = bf16[3,256,1,12,64]{1,4,3,0,2:T(8,128)(2,1)} fusion(bf16[3,256,12,64]{1,3,2,0:T(8,128)(2,1)} %reshape_reshape.13, f32[3,12,256,256]{2,3,1,0:T(8,128)} %copy-done.1, f32[3,12,256]{2,1,0:T(8,128)} %log_add_fusion), kind=kOutput, calls=%fused_computation.182 | convolution fusion | flops 309067776 | bytes 11833344 | tf_op jit(solution)/shard_map/ihqk,iqhe->ikhe/dot_general | solution.py:252
  368.5 8.2 %multiply_reduce_fusion = (f32[3,12,256]{2,1,0:T(8,128)}, f32[3,12,256,256]{2,3,1,0:T(8,128)}) fusion(f32[3,12,256,256]{2,3,1,0:T(8,128)} %copy-done.1, f32[3,12,256]{2,1,0:T(8,128)S(1)} %copy-done.46, bf16[3,256,12,64]{1,3,2,0:T(8,128)(2,1)S(1)} %copy-done.15, bf16[3,256,3,12,64]{1,4,3,2,0:T(8,128)(2,1)} %bitcast.310), kind=kOutput, calls=%fused_computation.54 | convolution fusion | flops 311417856 | bytes 21307392 | tf_op jit(solution)/shard_map/iqhe,ikhe->ihqk/dot_general | solution.py:251
  376.8 11.3 %multiply_convert_fusion = bf16[3,12,256,256]{2,3,1,0:T(8,128)(2,1)} fusion(f32[3,12,256,256]{2,3,1,0:T(8,128)} %get-tuple-element.170, f32[3,12,256,256]{2,3,1,0:T(8,128)} %copy-done.1, f32[3,12,256]{2,1,0:T(8,128)} %get-tuple-element.169, f32[3,12,256]{2,1,0:T(8,128)} %log_add_fusion), kind=kLoop, calls=%fused_computation.53 | loop fusion | flops 11796480 | bytes 23666688 | tf_op jit(solution)/shard_map/convert_element_type | solution.py:255
  404.3 5.3 bitcast_convert_fusion.2
  430.0 7.7 %fusion.78 = (bf16[768]{0:T(1024)(128)(2,1)}, bf16[768]{0:T(1024)(128)(2,1)}, bf16[768]{0:T(1024)(128)(2,1)}, bf16[768]{0:T(1024)(128)(2,1)S(1)}, bf16[768]{0:T(...) fusion(bf16[3,16,16,768]{3,2,1,0:T(8,128)(2,1)} %reshape.319, ...), kind=kLoop, calls=%fused_computation.144 | loop fusion | flops 18278400 | bytes 9596928 | tf_op jit(solution)/shard_map/reduce_sum | solution.py:87
  489.4 4.9 fusion.125
  494.3 5.7 fusion.134
  513.2 9.0 %collective-permute-done.15 = f32[4,3,4608]{2,1,0:T(4,128)S(1)} collective-permute-done((f32[4,3,4608]{2,1,0:T(4,128)S(1)}, f32[4,3,4608]{2,1,0:T(4,128)S(1)}, u32[]{:S(2)}, u32[]{:S(2)}) %collective-permute-start.15) | collective-permute-done | bytes 221216 | tf_op jit(solution)/shard_map/ppermute | solution.py:13
  549.5 7.4 %collective-permute-done.33 = bf16[2,2,96,768]{3,2,0,1:T(8,128)(2,1)S(1)} collective-permute-done((bf16[2,2,96,768]{3,2,0,1:T(8,128)(2,1)S(1)}, bf16[2,2,96,768]{3,2,0,1:T(8,128)(2,1)S(1)}, u32[]{:S(2)}, u32[]{:S(2)}) %collective-permute-start.33) | collective-permute-done | bytes 589856 | tf_op jit(solution)/shard_map/ppermute | solution.py:13
  566.9 5.4 collective-permute-done.35
  573.2 4.6 collective-permute-done.28
  (540 shorter events, 318.7 us)
Async XLA Ops:
  26.5 6.3 %collective-permute-start.1 = (bf16[3,1,18,768]{3,2,1,0:T(8,128)(2,1)S(1)}, bf16[3,1,18,768]{3,2,1,0:T(8,128)(2,1)S(1)}, u32[]{:S(2)}, u32[]{:S(2)}) collective-permute-start(bf16[3,1,18,768]{3,2,1,0:T(8,128)(2,1)S(1)} %fusion.121), channel_id=1, source_target_pairs={{0,2},{1,3},{2,0},{3,1},{4,6},{5,7},{6,4},{7,5},{8,10},{9,11},{10,... | collective-permute-start | bytes 248840 | tf_op jit(solution)/shard_map/ppermute | solution.py:13
  47.6 20.4 %all-to-all-start = ((bf16[3,4,64,768]{3,2,0,1:T(8,128)(2,1)}), bf16[3,4,64,768]{3,2,0,1:T(8,128)(2,1)}, u32[]{:S(2)}, u32[]{:S(2)}) async-start(bf16[3,4,64,768]{3,2,0,1:T(8,128)(2,1)} %bitcast.322), calls=%async_computation | async-start | bytes 2359296 | tf_op jit(solution)/shard_map/all_to_all | solution.py:96
  53.5 57.5 %collective-permute-start.10 = (bf16[1,3,768]{2,1,0:T(4,128)(2,1)}, bf16[1,3,768]{2,1,0:T(4,128)(2,1)}, u32[]{:S(2)}, u32[]{:S(2)}) collective-permute-start(bf16[1,3,768]{2,1,0:T(4,128)(2,1)} %fusion.163), channel_id=1, source_target_pairs={{0,4},{4,0},{8,12},{12,8},{16,20},{20,16},{24,28},{28,24},{1,5},{5... | collective-permute-start | bytes 13832 | tf_op jit(solution)/shard_map/ppermute | solution.py:13
  102.2 20.7 %all-to-all-start.1 = ((bf16[3,4,64,768]{3,2,0,1:T(8,128)(2,1)}), bf16[3,4,64,768]{3,2,0,1:T(8,128)(2,1)}, u32[]{:S(2)}, u32[]{:S(2)}) async-start(bf16[3,4,64,768]{3,2,0,1:T(8,128)(2,1)} %copy.110), calls=%async_computation.1 | async-start | bytes 2359296 | tf_op jit(solution)/shard_map/all_to_all | solution.py:103
  112.9 28.7 %collective-permute-start.11 = (bf16[2,3,768]{2,1,0:T(4,128)(2,1)}, bf16[2,3,768]{2,1,0:T(4,128)(2,1)}, u32[]{:S(2)}, u32[]{:S(2)}) collective-permute-start(bf16[2,3,768]{2,1,0:T(4,128)(2,1)} %pad_maximum_fusion.27), channel_id=1, source_target_pairs={{0,8},{4,12},{8,0},{12,4},{16,24},{20,28},{24,16},{28,20},{1,9},{5... | collective-permute-start | bytes 27656 | tf_op jit(solution)/shard_map/ppermute | solution.py:13
  148.0 12.6 %collective-permute-start.3 = (bf16[3,1,18,3072]{3,2,1,0:T(8,128)(2,1)}, bf16[3,1,18,3072]{3,2,1,0:T(8,128)(2,1)}, u32[]{:S(2)}, u32[]{:S(2)}) collective-permute-start(bf16[3,1,18,3072]{3,2,1,0:T(8,128)(2,1)} %fusion.110), channel_id=1, source_target_pairs={{0,2},{1,3},{2,0},{3,1},{4,6},{5,7},{6,4},{7,5},{8,10},{9,11},{10,... | collective-permute-start | bytes 995336 | tf_op jit(solution)/shard_map/ppermute | solution.py:13
  237.2 29.4 %collective-permute-start.5 = (bf16[3,1,18,3072]{3,2,1,0:T(8,128)(2,1)}, bf16[3,1,18,3072]{3,2,1,0:T(8,128)(2,1)}, u32[]{:S(2)}, u32[]{:S(2)}) collective-permute-start(bf16[3,1,18,3072]{3,2,1,0:T(8,128)(2,1)} %fusion.109), channel_id=1, source_target_pairs={{0,2},{1,3},{2,0},{3,1},{4,6},{5,7},{6,4},{7,5},{8,10},{9,11},{10,... | collective-permute-start | bytes 995336 | tf_op jit(solution)/shard_map/ppermute | solution.py:13
  266.4 146.1 %collective-permute-start.31 = (bf16[2,2,2,2,96,768]{5,4,0,1,2,3:T(8,128)(2,1)}, bf16[2,2,2,2,96,768]{5,4,0,1,2,3:T(8,128)(2,1)}, u32[]{:S(2)}, u32[]{:S(2)}) collective-permute-start(bf16[2,2,2,2,96,768]{5,4,0,1,2,3:T(8,128)(2,1)} %bitcast.295), channel_id=1, source_target_pairs={{0,1},{1,0},{2,3},{3,2},{4,5},{5,4},{6,7},{7,6},{8,9},{9,8},{10,11... | collective-permute-start | bytes 7077896 | tf_op jit(solution)/shard_map/ppermute | solution.py:13
  331.7 20.4 %all-to-all-start.2 = ((bf16[3,4,64,768]{3,2,0,1:T(8,128)(2,1)}), bf16[3,4,64,768]{3,2,0,1:T(8,128)(2,1)}, u32[]{:S(2)}, u32[]{:S(2)}) async-start(bf16[3,4,64,768]{3,2,0,1:T(8,128)(2,1)} %bitcast.321), calls=%async_computation.2 | async-start | bytes 2359296 | tf_op jit(solution)/shard_map/all_to_all | solution.py:96
  347.1 160.6 %collective-permute-start.26 = (bf16[2,2,2,2,24,3072]{5,4,0,1,3,2:T(8,128)(2,1)}, bf16[2,2,2,2,24,3072]{5,4,0,1,3,2:T(8,128)(2,1)}, u32[]{:S(2)}, u32[]{:S(2)}) collective-permute-start(bf16[2,2,2,2,24,3072]{5,4,0,1,3,2:T(8,128)(2,1)} %bitcast.296), channel_id=1, source_target_pairs={{0,1},{1,0},{2,3},{3,2},{4,5},{5,4},{6,7},{7,6},{8,9},{9,8},{10,11... | collective-permute-start | bytes 7077896 | tf_op jit(solution)/shard_map/ppermute | solution.py:13
  399.8 20.9 %all-to-all-start.3 = ((bf16[3,4,64,768]{3,2,0,1:T(8,128)(2,1)}), bf16[3,4,64,768]{3,2,0,1:T(8,128)(2,1)}, u32[]{:S(2)}, u32[]{:S(2)}) async-start(bf16[3,4,64,768]{3,2,0,1:T(8,128)(2,1)} %copy.127), calls=%async_computation.3 | async-start | bytes 2359296 | tf_op jit(solution)/shard_map/all_to_all | solution.py:103
  412.0 88.0 %collective-permute-start.16 = (bf16[2,2,2,2,24,1536]{5,4,3,2,1,0:T(8,128)(2,1)}, bf16[2,2,2,2,24,1536]{5,4,3,2,1,0:T(8,128)(2,1)}, u32[]{:S(2)}, u32[]{:S(2)}) collective-permute-start(bf16[2,2,2,2,24,1536]{5,4,3,2,1,0:T(8,128)(2,1)} %dynamic-slice_bitcast_fusion.2), channel_id=1, source_target_pairs={{0,1},{1,0},{2,3},{3,2},{4,5},{5,4},{6,7},{7,6},{8,9},{9,8},{10,11... | collective-permute-start | bytes 3538952 | tf_op jit(solution)/shard_map/ppermute | solution.py:13
  418.7 113.7 %collective-permute-start.32 = (bf16[2,2,2,96,768]{4,3,0,1,2:T(8,128)(2,1)}, bf16[2,2,2,96,768]{4,3,0,1,2:T(8,128)(2,1)}, u32[]{:S(2)}, u32[]{:S(2)}) collective-permute-start(bf16[2,2,2,96,768]{4,3,0,1,2:T(8,128)(2,1)} %dynamic-slice_bitcast_fusion), channel_id=1, source_target_pairs={{0,2},{1,3},{2,0},{3,1},{4,6},{5,7},{6,4},{7,5},{8,10},{9,11},{10,... | collective-permute-start | bytes 3538952 | tf_op jit(solution)/shard_map/ppermute | solution.py:13
  437.7 24.8 %collective-permute-start.6 = (bf16[3,16,1,768]{3,2,1,0:T(2,128)(2,1)}, bf16[3,16,1,768]{3,2,1,0:T(2,128)(2,1)}, u32[]{:S(2)}, u32[]{:S(2)}) collective-permute-start(bf16[3,16,1,768]{3,2,1,0:T(2,128)(2,1)} %broadcast_select_fusion.11), channel_id=1, source_target_pairs={{0,1},{1,0},{2,3},{3,2},{4,5},{5,4},{6,7},{7,6},{8,9},{9,8},{10,11... | collective-permute-start | bytes 221192 | tf_op jit(solution)/shard_map/ppermute | solution.py:13
  463.8 5.5 collective-permute-start.7
  466.5 72.2 %collective-permute-start.21 = (bf16[2,2,2,2,24,1664]{5,4,0,1,2,3:T(8,128)(2,1)}, bf16[2,2,2,2,24,1664]{5,4,0,1,2,3:T(8,128)(2,1)}, u32[]{:S(2)}, u32[]{:S(2)}) collective-permute-start(bf16[2,2,2,2,24,1664]{5,4,0,1,2,3:T(8,128)(2,1)} %bitcast.297), channel_id=1, source_target_pairs={{0,1},{1,0},{2,3},{3,2},{4,5},{5,4},{6,7},{7,6},{8,9},{9,8},{10,11... | collective-permute-start | bytes 3833864 | tf_op jit(solution)/shard_map/ppermute | solution.py:13
  487.8 13.8 %collective-permute-start.13 = (f32[1,3,4608]{2,1,0:T(4,128)S(1)}, f32[1,3,4608]{2,1,0:T(4,128)S(1)}, u32[]{:S(2)}, u32[]{:S(2)}) collective-permute-start(f32[1,3,4608]{2,1,0:T(4,128)S(1)} %bitcast.328), channel_id=1, source_target_pairs={{0,4},{4,0},{8,12},{12,8},{16,20},{20,16},{24,28},{28,24},{1,5},{5... | collective-permute-start | bytes 165896 | tf_op jit(solution)/shard_map/ppermute | solution.py:13
  501.7 5.4 collective-permute-start.14
  504.2 24.9 %collective-permute-start.17 = (bf16[2,2,2,24,1536]{4,3,2,1,0:T(8,128)(2,1)}, bf16[2,2,2,24,1536]{4,3,2,1,0:T(8,128)(2,1)}, u32[]{:S(2)}, u32[]{:S(2)}) collective-permute-start(bf16[2,2,2,24,1536]{4,3,2,1,0:T(8,128)(2,1)} %dynamic-slice_bitcast_fusion.6), channel_id=1, source_target_pairs={{0,4},{4,0},{8,12},{12,8},{16,20},{20,16},{24,28},{28,24},{1,5},{5... | collective-permute-start | bytes 1769480 | tf_op jit(solution)/shard_map/ppermute | solution.py:13
  507.3 15.0 %collective-permute-start.15 = (f32[4,3,4608]{2,1,0:T(4,128)S(1)}, f32[4,3,4608]{2,1,0:T(4,128)S(1)}, u32[]{:S(2)}, u32[]{:S(2)}) collective-permute-start(f32[4,3,4608]{2,1,0:T(4,128)S(1)} %pad_maximum_fusion.18), channel_id=1, source_target_pairs={{0,16},{4,20},{8,24},{12,28},{16,0},{20,4},{24,8},{28,12},{1,17},{... | collective-permute-start | bytes 663560 | tf_op jit(solution)/shard_map/ppermute | solution.py:13
  512.8 44.9 %collective-permute-start.27 = (bf16[2,2,2,24,3072]{4,3,0,1,2:T(8,128)(2,1)}, bf16[2,2,2,24,3072]{4,3,0,1,2:T(8,128)(2,1)}, u32[]{:S(2)}, u32[]{:S(2)}) collective-permute-start(bf16[2,2,2,24,3072]{4,3,0,1,2:T(8,128)(2,1)} %dynamic-slice_bitcast_fusion.1), channel_id=1, source_target_pairs={{0,4},{4,0},{8,12},{12,8},{16,20},{20,16},{24,28},{28,24},{1,5},{5... | collective-permute-start | bytes 3538952 | tf_op jit(solution)/shard_map/ppermute | solution.py:13
  530.6 8.0 %collective-permute-start.18 = (bf16[2,2,24,1536]{3,2,1,0:T(8,128)(2,1)S(1)}, bf16[2,2,24,1536]{3,2,1,0:T(8,128)(2,1)S(1)}, u32[]{:S(2)}, u32[]{:S(2)}) collective-permute-start(bf16[2,2,24,1536]{3,2,1,0:T(8,128)(2,1)S(1)} %dynamic-slice_bitcast_fusion.10), channel_id=1, source_target_pairs={{0,2},{1,3},{2,0},{3,1},{4,6},{5,7},{6,4},{7,5},{8,10},{9,11},{10,... | collective-permute-start | bytes 884744 | tf_op jit(solution)/shard_map/ppermute | solution.py:13
  534.0 23.0 %collective-permute-start.33 = (bf16[2,2,96,768]{3,2,0,1:T(8,128)(2,1)S(1)}, bf16[2,2,96,768]{3,2,0,1:T(8,128)(2,1)S(1)}, u32[]{:S(2)}, u32[]{:S(2)}) collective-permute-start(bf16[2,2,96,768]{3,2,0,1:T(8,128)(2,1)S(1)} %dynamic-slice_bitcast_fusion.4), channel_id=1, source_target_pairs={{0,4},{4,0},{8,12},{12,8},{16,20},{20,16},{24,28},{28,24},{1,5},{5... | collective-permute-start | bytes 1769480 | tf_op jit(solution)/shard_map/ppermute | solution.py:13
  543.9 5.6 collective-permute-start.20
  545.0 14.9 %collective-permute-start.22 = (bf16[2,2,2,24,1664]{4,3,0,1,2:T(8,128)(2,1)S(1)}, bf16[2,2,2,24,1664]{4,3,0,1,2:T(8,128)(2,1)S(1)}, u32[]{:S(2)}, u32[]{:S(2)}) collective-permute-start(bf16[2,2,2,24,1664]{4,3,0,1,2:T(8,128)(2,1)S(1)} %dynamic-slice_bitcast_fusion.3), channel_id=1, source_target_pairs={{0,2},{1,3},{2,0},{3,1},{4,6},{5,7},{6,4},{7,5},{8,10},{9,11},{10,... | collective-permute-start | bytes 1916936 | tf_op jit(solution)/shard_map/ppermute | solution.py:13
  557.1 7.5 %collective-permute-start.34 = (bf16[2,96,768]{2,1,0:T(8,128)(2,1)S(1)}, bf16[2,96,768]{2,1,0:T(8,128)(2,1)S(1)}, u32[]{:S(2)}, u32[]{:S(2)}) collective-permute-start(bf16[2,96,768]{2,1,0:T(8,128)(2,1)S(1)} %dynamic-slice_bitcast_fusion.8), channel_id=1, source_target_pairs={{0,8},{4,12},{8,0},{12,4},{16,24},{20,28},{24,16},{28,20},{1,9},{5... | collective-permute-start | bytes 884744 | tf_op jit(solution)/shard_map/ppermute | solution.py:13
  560.1 12.9 %collective-permute-start.23 = (bf16[2,2,24,1664]{3,2,0,1:T(8,128)(2,1)S(1)}, bf16[2,2,24,1664]{3,2,0,1:T(8,128)(2,1)S(1)}, u32[]{:S(2)}, u32[]{:S(2)}) collective-permute-start(bf16[2,2,24,1664]{3,2,0,1:T(8,128)(2,1)S(1)} %dynamic-slice_bitcast_fusion.7), channel_id=1, source_target_pairs={{0,4},{4,0},{8,12},{12,8},{16,20},{20,16},{24,28},{28,24},{1,5},{5... | collective-permute-start | bytes 958472 | tf_op jit(solution)/shard_map/ppermute | solution.py:13
  564.7 7.6 %collective-permute-start.35 = (bf16[96,768]{1,0:T(8,128)(2,1)S(1)}, bf16[96,768]{1,0:T(8,128)(2,1)S(1)}, u32[]{:S(2)}, u32[]{:S(2)}) collective-permute-start(bf16[96,768]{1,0:T(8,128)(2,1)S(1)} %dynamic-slice_bitcast_fusion.12), channel_id=1, source_target_pairs={{0,16},{4,20},{8,24},{12,28},{16,0},{20,4},{24,8},{28,12},{1,17},{... | collective-permute-start | bytes 442376 | tf_op jit(solution)/shard_map/ppermute | solution.py:13
  565.2 12.6 %collective-permute-start.28 = (bf16[2,2,24,3072]{3,2,0,1:T(8,128)(2,1)S(1)}, bf16[2,2,24,3072]{3,2,0,1:T(8,128)(2,1)S(1)}, u32[]{:S(2)}, u32[]{:S(2)}) collective-permute-start(bf16[2,2,24,3072]{3,2,0,1:T(8,128)(2,1)S(1)} %dynamic-slice_bitcast_fusion.5), channel_id=1, source_target_pairs={{0,2},{1,3},{2,0},{3,1},{4,6},{5,7},{6,4},{7,5},{8,10},{9,11},{10,... | collective-permute-start | bytes 1769480 | tf_op jit(solution)/shard_map/ppermute | solution.py:13
  578.6 5.7 collective-permute-start.25
  580.7 6.8 %collective-permute-start.29 = (bf16[2,24,3072]{2,1,0:T(8,128)(2,1)S(1)}, bf16[2,24,3072]{2,1,0:T(8,128)(2,1)S(1)}, u32[]{:S(2)}, u32[]{:S(2)}) collective-permute-start(bf16[2,24,3072]{2,1,0:T(8,128)(2,1)S(1)} %dynamic-slice_bitcast_fusion.9), channel_id=1, source_target_pairs={{0,8},{4,12},{8,0},{12,4},{16,24},{20,28},{24,16},{28,20},{1,9},{5... | collective-permute-start | bytes 884744 | tf_op jit(solution)/shard_map/ppermute | solution.py:13
  589.0 7.9 %collective-permute-start.30 = (bf16[24,3072]{1,0:T(8,128)(2,1)}, bf16[24,3072]{1,0:T(8,128)(2,1)}, u32[]{:S(2)}, u32[]{:S(2)}) collective-permute-start(bf16[24,3072]{1,0:T(8,128)(2,1)} %dynamic-slice_bitcast_fusion.13), channel_id=1, source_target_pairs={{0,16},{4,20},{8,24},{12,28},{16,0},{20,4},{24,8},{28,12},{1,17},{... | collective-permute-start | bytes 442376 | tf_op jit(solution)/shard_map/ppermute | solution.py:13
  (148 other events, 1106.3 us)
where the time goes:
time: 608 us; the launch traced here: 599 us
  other arithmetic  158 us (26%)
  local copies, waits for them, and re-layouts  151 us (25%)
  matrix products  145 us (24%)
  waiting for transfers between devices  91.6 us (15%)
  starting transfers between devices  49.7 us (8%)
    ppermute x36, waiting for transfers between devices, from_partner(): lax.ppermute(shard, axis, [(i, i ^ 1 << bit) for i in range(lax.axis_size...  69.2 us
    dot_general x1, matrix products, shards(): jnp.einsum('ixyd,fd->ixyf', d_branch_two, w_down, preferred_element_type=...  35.1 us
    ppermute x36, starting transfers between devices, from_partner(): lax.ppermute(shard, axis, [(i, i ^ 1 << bit) for i in range(lax.axis_size...  31.4 us
    concatenate x4, other arithmetic, extend(): return jnp.concatenate([top_rim, widened, bottom_rim], 1)  27.2 us
    unnamed x288, local copies, waits for them, and re-layouts  22.7 us
    another operation x22, local copies, waits for them, and re-layouts, tap_grads(): return jnp.stack(columns, 1)  19.4 us
    convert_element_type x1, other arithmetic, shards(): apply_taps(d_padded_ffn, conv_ffn, half_side, True).astype(jnp.bfloat16)  15.8 us
    add x1, other arithmetic, apply_taps(): summed = summed + window * weights_f[:, stencil]  15.6 us
  transfers between devices with their start and end apart: 40, of which 22 were waited for; matrix products, arithmetic and copies ran while one was open for 55% of the time, Pallas kernels for 0%

commit v1 on v0

--- a/solution.py
+++ b/solution.py
@@ -7,6 +7,22 @@
 HEADS = 12
 HEAD_DIM = 64
 epsilon = 1e-06
+
+
+def point_cube(u_in, pos_dim, patch):
+    tile_out, upper = (u_in.shape[:pos_dim], u_in.shape[pos_dim + 1 :])
+    block_out = u_in.reshape(*tile_out, patch, -1, *upper)
+    current_block = jnp.moveaxis(block_out, pos_dim, 0)
+    return current_block
+
+
+def process_kinds_for(block_in, at_axis):
+    block_in = jnp.moveaxis(block_in, 0, at_axis)
+    field_out = block_in.shape
+    small = block_in.reshape(
+        *field_out[:at_axis], field_out[at_axis] * field_out[at_axis + 1], *field_out[at_axis + 2 :]
+    )
+    return small
 
 
 def from_partner(shard, axis, bit):
@@ -93,7 +109,21 @@
     quarter = side_len // 2
     pieces = field_map.reshape(count, quarter, 2, quarter, 2, channels).transpose(0, 2, 4, 1, 3, 5)
     pieces = pieces.reshape(count, 4, quarter * quarter, channels)
-    incoming = lax.all_to_all(pieces, "narrow", split_axis=1, concat_axis=1, tiled=True)
+
+    def refer_tiles_by_axis(point, axis_tag, s0, w_in):
+        raw_out = jax.lax.axis_size(axis_tag)
+        v_next, mixed_arr = (raw_out, jax.lax.axis_index(axis_tag))
+        t1 = point_cube(point, s0, v_next)
+        seen = [t1[mixed_arr]]
+        for ii in range(1, v_next):
+            y2 = t1[mixed_arr ^ ii]
+            found_now = jax.lax.ppermute(y2, axis_tag, [(q, q ^ ii) for q in range(v_next)])
+            seen.append(found_now)
+        t1 = jnp.stack(seen, 0)[mixed_arr ^ jnp.arange(v_next)]
+        local_next = process_kinds_for(t1, w_in)
+        return local_next
+
+    incoming = refer_tiles_by_axis(pieces, "narrow", 1, 1)
     return incoming.reshape(count, 4 * quarter * quarter, channels)
 
 

time: 608 us -> 642 us (1.056)
  waiting for transfers between devices: 91.6 us -> 127 us
    ppermute x36, waiting for transfers between devices: 69.2 us -> 94 us  [from_partner(): lax.ppermute(shard, axis, [(i, i ^ 1 << bit) for i in range(lax.axis_size...]
    ppermute x0 -> x6, waiting for transfers between devices: none -> 18.2 us  [refer_tiles_by_axis(): jax.lax.ppermute(y2, axis_tag, [(q, q ^ ii) for q in range(v_next)])]
    all_to_all x2 -> x0, waiting for transfers between devices: 14.2 us -> none  [to_groups(): lax.all_to_all(pieces, 'narrow', split_axis=1, concat_axis=1, tiled=True)]
    all_to_all x2 -> x0, starting transfers between devices: 9.02 us -> none  [to_groups(): lax.all_to_all(pieces, 'narrow', split_axis=1, concat_axis=1, tiled=True)]
    all_to_all x2 -> x0, local copies, waits for them, and re-layouts: 6.51 us -> none  [to_groups(): lax.all_to_all(pieces, 'narrow', split_axis=1, concat_axis=1, tiled=True)]
    unnamed x288 -> x296, local copies, waits for them, and re-layouts: 22.7 us -> 19.5 us
  transfers between devices with their start and end apart: 40 -> 44, of which waited for: 22 -> 19; matrix products, arithmetic and copies ran while one was open for 55% -> 53% of each run, Pallas kernels for 0% -> 0%
where the time goes in v1:
time: 642 us; the launch traced here: 635 us
  other arithmetic  162 us (25%)
  local copies, waits for them, and re-layouts  149 us (23%)
  matrix products  146 us (23%)
  waiting for transfers between devices  127 us (20%)
  starting transfers between devices  48.1 us (7%)
    ppermute x36, waiting for transfers between devices, from_partner(): lax.ppermute(shard, axis, [(i, i ^ 1 << bit) for i in range(lax.axis_size...  94 us
    dot_general x1, matrix products, shards(): jnp.einsum('ixyd,fd->ixyf', d_branch_two, w_down, preferred_element_type=...  35.4 us
    ppermute x36, starting transfers between devices, from_partner(): lax.ppermute(shard, axis, [(i, i ^ 1 << bit) for i in range(lax.axis_size...  34.9 us
    concatenate x4, other arithmetic, extend(): return jnp.concatenate([top_rim, widened, bottom_rim], 1)  27.5 us
    unnamed x296, local copies, waits for them, and re-layouts  19.5 us
    another operation x22, local copies, waits for them, and re-layouts, tap_grads(): return jnp.stack(columns, 1)  19.4 us
    ppermute x6, waiting for transfers between devices, refer_tiles_by_axis(): jax.lax.ppermute(y2, axis_tag, [(q, q ^ ii) for q in range(v_next)])  18.2 us
    convert_element_type x1, other arithmetic, shards(): apply_taps(d_padded_ffn, conv_ffn, half_side, True).astype(jnp.bfloat16)  16 us
  transfers between devices with their start and end apart: 44, of which 19 were waited for; matrix products, arithmetic and copies ran while one was open for 53% of the time, Pallas kernels for 0%

profile of v1, /device:TPU:0, one launch (start us, length us, event | category | flops | bytes accessed | tf_op | source)
XLA Modules:
  0.0 635.1 jit_solution(355455117903117123)
XLA Ops:
  56.2 6.6 %collective-permute-done.3 = bf16[3,1,64,768]{3,2,0,1:T(8,128)(2,1)S(1)} collective-permute-done((bf16[3,1,64,768]{3,2,0,1:T(8,128)(2,1)S(1)}, bf16[3,1,64,768]{3,2,0,1:T(8,128)(2,1)S(1)}, u32[]{:S(2)}, u32[]{:S(2)}) %collective-permute-start.3) | collective-permute-done | bytes 294944 | tf_op jit(solution)/shard_map/ppermute | solution.py:120
  73.6 5.8 copy.106
  95.9 5.1 copy.111
  113.5 8.2 %all-to-all-done = bf16[3,4,64,768]{3,2,0,1:T(8,128)(2,1)} async-done(((bf16[3,4,64,768]{3,2,0,1:T(8,128)(2,1)}), bf16[3,4,64,768]{3,2,0,1:T(8,128)(2,1)}, u32[]{:S(2)}, u32[]{:S(2)}) %all-to-all-start) | async-done | bytes 1179680 | tf_op jit(solution)/shard_map/all_to_all | solution.py:133
  128.9 5.0 fusion.143
  148.7 10.8 %collective-permute-done.6 = bf16[3,1,18,3072]{3,2,1,0:T(8,128)(2,1)} collective-permute-done((bf16[3,1,18,3072]{3,2,1,0:T(8,128)(2,1)}, bf16[3,1,18,3072]{3,2,1,0:T(8,128)(2,1)}, u32[]{:S(2)}, u32[]{:S(2)}) %collective-permute-start.6) | collective-permute-done | bytes 331808 | tf_op jit(solution)/shard_map/ppermute | solution.py:29
  160.6 12.1 %maximum_maximum_fusion = (bf16[3,17,18,3072]{3,2,1,0:T(8,128)(2,1)S(1)}, bf16[3,17,18,3072]{3,2,1,0:T(8,128)(2,1)S(1)}) fusion(bf16[3,16,1,3072]{3,2,1,0:T(2,128)(2,1)} %copy-done.25, bf16[3,16,16,3072]{3,2,1,0:T(8,128)(2,1)} %copy-done.5, bf16[3,16,1,3072]{3,2,1,0:T(2,128)(2,1)} %copy-done.23, bf16[3,1,18,3072]{3,2,1,0:T(8,128)(2,1)S(1)} %get-tuple-element.129, ...), kind=kLoop, calls=%fused_computation.63 | loop fusion | flops 45121536 | bytes 17252352 | tf_op jit(solution)/shard_map/concatenate | solution.py:75
  172.9 15.6 %fusion.7 = f32[3,16,16,3072]{3,2,1,0:T(8,128)} fusion(bf16[3,16,16,3072]{3,2,1,0:T(8,128)(2,1)S(1)} %bitcast.342, bf16[3,16,1,3072]{3,2,1,0:T(2,128)(2,1)} %copy-done.25, bf16[3,16,1,3072]{3,2,1,0:T(2,128)(2,1)S(1)} %copy-done.24, f32[3072]{0:T(1024)S(1)} %bitcast.396, f32[3072]{0:T(1024)S(1)} %bitcast.394, f32[3072]{0:T(1024)S(1)} %bitcast.392, ...), kind=kLoop, calls=%fused_computation.30 | loop fusion | flops 75497472 | bytes 43167744 | tf_op jit(solution)/shard_map/add | solution.py:90
  188.5 35.4 %fusion.29 = (bf16[3072]{0:T(1024)(128)(2,1)}, bf16[3072]{0:T(1024)(128)(2,1)}, bf16[3072]{0:T(1024)(128)(2,1)}, bf16[3072]{0:T(1024)(128)(2,1)}, bf16[3072]{0:T...) fusion(bf16[3,17,18,3072]{3,2,1,0:T(8,128)(2,1)} %copy-done.4, ...), kind=kOutput, calls=%fused_computation.52 | convolution fusion | flops 3753612288 | bytes 53738508 | tf_op jit(solution)/shard_map/ixyd,fd->ixyf/dot_general | solution.py:255
  236.8 9.7 %bitcast_convert_fusion = bf16[3072,768]{1,0:T(8,128)(2,1)} fusion(bf16[3,16,16,768]{3,2,1,0:T(8,128)(2,1)S(1)} %bitcast.401, f32[3]{0:T(128)S(1)} %compare_convert_fusion, f32[3,768]{1,0:T(4,128)S(1)} %copy-done.115, f32[3,16,16,3072]{3,2,1,0:T(8,128)} %fusion.7), kind=kOutput, calls=%fused_computation.53 | convolution fusion | flops 3649830912 | bytes 15344652 | tf_op jit(solution)/shard_map/ixyf,ixyd->fd/dot_general | solution.py:252
  267.0 10.0 %pad_maximum_fusion.1 = (bf16[3,17,18,3072]{3,2,1,0:T(8,128)(2,1)S(1)}, bf16[3,17,18,3072]{3,2,1,0:T(8,128)(2,1)S(1)}) fusion(bf16[3,1,18,3072]{3,2,1,0:T(8,128)(2,1)S(1)} %get-tuple-element.127, bf16[3,16,1,3072]{3,2,1,0:T(2,128)(2,1)S(1)} %copy-done.29, bf16[3,16,16,3072]{3,2,1,0:T(8,128)(2,1)S(1)} %bitcast.340, ...), kind=kLoop, calls=%fused_computation.65 | loop fusion | flops 45121536 | bytes 17252352 | tf_op jit(solution)/shard_map/concatenate | solution.py:75
  277.1 16.0 %fusion.20 = bf16[3,16,16,3072]{3,2,1,0:T(8,128)(2,1)} fusion(bf16[3,16,16,3072]{3,2,1,0:T(8,128)(2,1)S(1)} %bitcast.340, bf16[3,17,18,3072]{3,2,1,0:T(8,128)(2,1)S(1)} %get-tuple-element.100, bf16[3,16,1,3072]{3,2,1,0:T(2,128)(2,1)S(1)} %copy-done.27, bf16[3,16,1,3072]{3,2,1,0:T(2,128)(2,1)} %copy-done.28, ...), kind=kLoop, calls=%fused_computation.43 | loop fusion | flops 77856768 | bytes 38449152 | tf_op jit(solution)/shard_map/convert_element_type | solution.py:265
  293.2 8.6 %multiply_reduce_fusion.5 = (f32[3,16,16]{2,1,0:T(8,128)S(1)}, f32[3,16,16,768]{3,2,1,0:T(8,128)S(1)}) fusion(f32[3,16,16,768]{3,2,1,0:T(8,128)} %copy-done.12, f32[3,768]{1,0:T(4,128)S(1)} %copy-done.95, f32[3,16,16]{2,1,0:T(8,128)S(1)} %copy-done.54, bf16[3,16,16,3072]{3,2,1,0:T(8,128)(2,1)} %fusion.20, bf16[768,3072]{1,0:T(8,128)(2,1)} %param.17), kind=kOutput, calls=%fused_computation.172 | convolution fusion | flops 3626237184 | bytes 14171136 | tf_op jit(solution)/shard_map/ixyf,df->ixyd/dot_general | solution.py:267
  303.9 11.7 %fusion.86 = (f32[3,768]{1,0:T(4,128)}, bf16[3,16,16,768]{3,2,1,0:T(8,128)(2,1)}, f32[3,768]{1,0:T(4,128)}, f32[3,16,16,768]{3,2,1,0:T(8,128)S(1)}) fusion(bf16[3,16,16,768]{3,2,1,0:T(8,128)(2,1)S(1)} %bitcast.402, f32[3]{0:T(128)S(1)} %compare_convert_fusion, f32[3,16,16,768]{3,2,1,0:T(8,128)S(1)} %copy-done.13, f32[3,768]{1,0:T(4,128)S(1)} %copy-done.116, ...), kind=kOutput, calls=%fused_computation.161 | convolution fusion | flops 3655724544 | bytes 26001420 | tf_op jit(solution)/shard_map/dot_general | solution.py:245
  319.9 6.4 %bitcast_convert_fusion.1 = bf16[768,3072]{1,0:T(8,128)(2,1)} fusion(bf16[3,16,16,3072]{3,2,1,0:T(8,128)(2,1)S(1)} %bitcast.351, f32[3,16,16,768]{3,2,1,0:T(8,128)S(1)} %copy-done.13, f32[3,768]{1,0:T(4,128)S(1)} %copy-done.118, f32[3,768]{1,0:T(4,128)S(1)} %copy-done.95, f32[3,16,16]{2,1,0:T(8,128)S(1)} %copy-done.82, f32[3,16,16]{2,1,0:T(8,128)S(1)} %copy-done.54), kind=kOutput, calls=%fused_computation.54 | convolution fusion | flops 3629187072 | bytes 11821056 | tf_op jit(solution)/shard_map/ixyd,ixyf->df/dot_general | solution.py:266
  340.8 6.7 %collective-permute-done.10 = bf16[3,1,64,768]{3,2,0,1:T(8,128)(2,1)S(1)} collective-permute-done((bf16[3,1,64,768]{3,2,0,1:T(8,128)(2,1)S(1)}, bf16[3,1,64,768]{3,2,0,1:T(8,128)(2,1)S(1)}, u32[]{:S(2)}, u32[]{:S(2)}) %collective-permute-start.10) | collective-permute-done | bytes 294944 | tf_op jit(solution)/shard_map/ppermute | solution.py:120
  351.7 5.1 copy.121
  361.4 6.8 %fusion.87 = bf16[3,256,1,12,64]{1,4,3,0,2:T(8,128)(2,1)} fusion(bf16[3,256,12,64]{1,3,2,0:T(8,128)(2,1)} %reshape_reshape_reshape.3, f32[3,12,256,256]{2,3,1,0:T(8,128)} %copy-done.1, f32[3,12,256]{2,1,0:T(8,128)} %log_add_fusion), kind=kOutput, calls=%fused_computation.184 | convolution fusion | flops 309067776 | bytes 11833344 | tf_op jit(solution)/shard_map/ihqk,iqhe->ikhe/dot_general | solution.py:282
  368.2 8.3 %multiply_reduce_fusion = (f32[3,12,256]{2,1,0:T(8,128)}, f32[3,12,256,256]{2,3,1,0:T(8,128)}) fusion(f32[3,12,256,256]{2,3,1,0:T(8,128)} %copy-done.1, f32[3,12,256]{2,1,0:T(8,128)S(1)} %copy-done.46, bf16[3,256,12,64]{1,3,2,0:T(8,128)(2,1)S(1)} %copy-done.15, bf16[3,256,3,12,64]{1,4,3,2,0:T(8,128)(2,1)} %bitcast.345), kind=kOutput, calls=%fused_computation.56 | convolution fusion | flops 311417856 | bytes 21307392 | tf_op jit(solution)/shard_map/iqhe,ikhe->ihqk/dot_general | solution.py:281
  376.5 11.3 %multiply_convert_fusion = bf16[3,12,256,256]{2,3,1,0:T(8,128)(2,1)} fusion(f32[3,12,256,256]{2,3,1,0:T(8,128)} %get-tuple-element.178, f32[3,12,256,256]{2,3,1,0:T(8,128)} %copy-done.1, f32[3,12,256]{2,1,0:T(8,128)} %get-tuple-element.177, f32[3,12,256]{2,1,0:T(8,128)} %log_add_fusion), kind=kLoop, calls=%fused_computation.55 | loop fusion | flops 11796480 | bytes 23666688 | tf_op jit(solution)/shard_map/convert_element_type | solution.py:285
  404.0 5.3 bitcast_convert_fusion.2
  413.6 6.3 all-to-all-done.1
  429.3 7.6 %fusion.78 = (bf16[768]{0:T(1024)(128)(2,1)}, bf16[768]{0:T(1024)(128)(2,1)}, bf16[768]{0:T(1024)(128)(2,1)}, bf16[768]{0:T(1024)(128)(2,1)S(1)}, bf16[768]{0:T(...) fusion(bf16[3,16,16,768]{3,2,1,0:T(8,128)(2,1)} %reshape.337, ...), kind=kLoop, calls=%fused_computation.146 | loop fusion | flops 18278400 | bytes 9596928 | tf_op jit(solution)/shard_map/reduce_sum | solution.py:103
  488.5 4.9 fusion.125
  493.4 5.7 fusion.134
  513.3 8.0 %collective-permute-done.21 = f32[4,3,4608]{2,1,0:T(4,128)S(1)} collective-permute-done((f32[4,3,4608]{2,1,0:T(4,128)S(1)}, f32[4,3,4608]{2,1,0:T(4,128)S(1)}, u32[]{:S(2)}, u32[]{:S(2)}) %collective-permute-start.21) | collective-permute-done | bytes 221216 | tf_op jit(solution)/shard_map/ppermute | solution.py:29
  530.5 14.1 %collective-permute-done.24 = bf16[2,2,24,1536]{3,2,1,0:T(8,128)(2,1)S(1)} collective-permute-done((bf16[2,2,24,1536]{3,2,1,0:T(8,128)(2,1)S(1)}, bf16[2,2,24,1536]{3,2,1,0:T(8,128)(2,1)S(1)}, u32[]{:S(2)}, u32[]{:S(2)}) %collective-permute-start.24) | collective-permute-done | bytes 294944 | tf_op jit(solution)/shard_map/ppermute | solution.py:29
  559.1 5.2 collective-permute-done.28
  568.3 22.6 %collective-permute-done.29 = bf16[2,2,24,1664]{3,2,0,1:T(8,128)(2,1)S(1)} collective-permute-done((bf16[2,2,24,1664]{3,2,0,1:T(8,128)(2,1)S(1)}, bf16[2,2,24,1664]{3,2,0,1:T(8,128)(2,1)S(1)}, u32[]{:S(2)}, u32[]{:S(2)}) %collective-permute-start.29) | collective-permute-done | bytes 319520 | tf_op jit(solution)/shard_map/ppermute | solution.py:29
  591.5 7.8 %collective-permute-done.39 = bf16[2,2,96,768]{3,2,0,1:T(8,128)(2,1)S(1)} collective-permute-done((bf16[2,2,96,768]{3,2,0,1:T(8,128)(2,1)S(1)}, bf16[2,2,96,768]{3,2,0,1:T(8,128)(2,1)S(1)}, u32[]{:S(2)}, u32[]{:S(2)}) %collective-permute-start.39) | collective-permute-done | bytes 589856 | tf_op jit(solution)/shard_map/ppermute | solution.py:29
  620.4 6.0 collective-permute-done.35
  628.3 5.9 collective-permute-done.36
  (564 shorter events, 326.7 us)
Async XLA Ops:
  47.1 9.1 %collective-permute-start.4 = (bf16[3,1,64,768]{3,2,0,1:T(8,128)(2,1)S(1)}, bf16[3,1,64,768]{3,2,0,1:T(8,128)(2,1)S(1)}, u32[]{:S(2)}, u32[]{:S(2)}) collective-permute-start(bf16[3,1,64,768]{3,2,0,1:T(8,128)(2,1)S(1)} %get-tuple-element.122), channel_id=1, source_target_pairs={{0,3},{1,2},{2,1},{3,0},{4,7},{5,6},{6,5},{7,4},{8,11},{9,10},{10,... | collective-permute-start | bytes 884744 | tf_op jit(solution)/shard_map/ppermute | solution.py:120
  47.8 14.9 %collective-permute-start.3 = (bf16[3,1,64,768]{3,2,0,1:T(8,128)(2,1)S(1)}, bf16[3,1,64,768]{3,2,0,1:T(8,128)(2,1)S(1)}, u32[]{:S(2)}, u32[]{:S(2)}) collective-permute-start(bf16[3,1,64,768]{3,2,0,1:T(8,128)(2,1)S(1)} %get-tuple-element.123), channel_id=1, source_target_pairs={{0,2},{1,3},{2,0},{3,1},{4,6},{5,7},{6,4},{7,5},{8,10},{9,11},{10,... | collective-permute-start | bytes 884744 | tf_op jit(solution)/shard_map/ppermute | solution.py:120
  49.0 13.8 %collective-permute-start.2 = (bf16[3,1,64,768]{3,2,0,1:T(8,128)(2,1)S(1)}, bf16[3,1,64,768]{3,2,0,1:T(8,128)(2,1)S(1)}, u32[]{:S(2)}, u32[]{:S(2)}) collective-permute-start(bf16[3,1,64,768]{3,2,0,1:T(8,128)(2,1)S(1)} %get-tuple-element.124), channel_id=1, source_target_pairs={{0,1},{1,0},{2,3},{3,2},{4,5},{5,4},{6,7},{7,6},{8,9},{9,8},{10,11... | collective-permute-start | bytes 884744 | tf_op jit(solution)/shard_map/ppermute | solution.py:120
  49.6 60.1 %collective-permute-start.16 = (bf16[1,3,768]{2,1,0:T(4,128)(2,1)}, bf16[1,3,768]{2,1,0:T(4,128)(2,1)}, u32[]{:S(2)}, u32[]{:S(2)}) collective-permute-start(bf16[1,3,768]{2,1,0:T(4,128)(2,1)} %fusion.164), channel_id=1, source_target_pairs={{0,4},{4,0},{8,12},{12,8},{16,20},{20,16},{24,28},{28,24},{1,5},{5... | collective-permute-start | bytes 13832 | tf_op jit(solution)/shard_map/ppermute | solution.py:29
  101.0 20.7 %all-to-all-start = ((bf16[3,4,64,768]{3,2,0,1:T(8,128)(2,1)}), bf16[3,4,64,768]{3,2,0,1:T(8,128)(2,1)}, u32[]{:S(2)}, u32[]{:S(2)}) async-start(bf16[3,4,64,768]{3,2,0,1:T(8,128)(2,1)} %copy.111), calls=%async_computation | async-start | bytes 2359296 | tf_op jit(solution)/shard_map/all_to_all | solution.py:133
  111.7 28.7 %collective-permute-start.17 = (bf16[2,3,768]{2,1,0:T(4,128)(2,1)}, bf16[2,3,768]{2,1,0:T(4,128)(2,1)}, u32[]{:S(2)}, u32[]{:S(2)}) collective-permute-start(bf16[2,3,768]{2,1,0:T(4,128)(2,1)} %pad_maximum_fusion.27), channel_id=1, source_target_pairs={{0,8},{4,12},{8,0},{12,4},{16,24},{20,28},{24,16},{28,20},{1,9},{5... | collective-permute-start | bytes 27656 | tf_op jit(solution)/shard_map/ppermute | solution.py:29
  146.8 12.6 %collective-permute-start.6 = (bf16[3,1,18,3072]{3,2,1,0:T(8,128)(2,1)}, bf16[3,1,18,3072]{3,2,1,0:T(8,128)(2,1)}, u32[]{:S(2)}, u32[]{:S(2)}) collective-permute-start(bf16[3,1,18,3072]{3,2,1,0:T(8,128)(2,1)} %fusion.110), channel_id=1, source_target_pairs={{0,2},{1,3},{2,0},{3,1},{4,6},{5,7},{6,4},{7,5},{8,10},{9,11},{10,... | collective-permute-start | bytes 995336 | tf_op jit(solution)/shard_map/ppermute | solution.py:29
  236.3 29.5 %collective-permute-start.8 = (bf16[3,1,18,3072]{3,2,1,0:T(8,128)(2,1)}, bf16[3,1,18,3072]{3,2,1,0:T(8,128)(2,1)}, u32[]{:S(2)}, u32[]{:S(2)}) collective-permute-start(bf16[3,1,18,3072]{3,2,1,0:T(8,128)(2,1)} %fusion.109), channel_id=1, source_target_pairs={{0,2},{1,3},{2,0},{3,1},{4,6},{5,7},{6,4},{7,5},{8,10},{9,11},{10,... | collective-permute-start | bytes 995336 | tf_op jit(solution)/shard_map/ppermute | solution.py:29
  265.6 241.2 %collective-permute-start.37 = (bf16[2,2,2,2,96,768]{5,4,0,1,2,3:T(8,128)(2,1)}, bf16[2,2,2,2,96,768]{5,4,0,1,2,3:T(8,128)(2,1)}, u32[]{:S(2)}, u32[]{:S(2)}) collective-permute-start(bf16[2,2,2,2,96,768]{5,4,0,1,2,3:T(8,128)(2,1)} %bitcast.330), channel_id=1, source_target_pairs={{0,1},{1,0},{2,3},{3,2},{4,5},{5,4},{6,7},{7,6},{8,9},{9,8},{10,11... | collective-permute-start | bytes 7077896 | tf_op jit(solution)/shard_map/ppermute | solution.py:29
  331.8 9.0 %collective-permute-start.11 = (bf16[3,1,64,768]{3,2,0,1:T(8,128)(2,1)S(1)}, bf16[3,1,64,768]{3,2,0,1:T(8,128)(2,1)S(1)}, u32[]{:S(2)}, u32[]{:S(2)}) collective-permute-start(bf16[3,1,64,768]{3,2,0,1:T(8,128)(2,1)S(1)} %get-tuple-element.118), channel_id=1, source_target_pairs={{0,3},{1,2},{2,1},{3,0},{4,7},{5,6},{6,5},{7,4},{8,11},{9,10},{10,... | collective-permute-start | bytes 884744 | tf_op jit(solution)/shard_map/ppermute | solution.py:120
  333.4 14.1 %collective-permute-start.10 = (bf16[3,1,64,768]{3,2,0,1:T(8,128)(2,1)S(1)}, bf16[3,1,64,768]{3,2,0,1:T(8,128)(2,1)S(1)}, u32[]{:S(2)}, u32[]{:S(2)}) collective-permute-start(bf16[3,1,64,768]{3,2,0,1:T(8,128)(2,1)S(1)} %get-tuple-element.119), channel_id=1, source_target_pairs={{0,2},{1,3},{2,0},{3,1},{4,6},{5,7},{6,4},{7,5},{8,10},{9,11},{10,... | collective-permute-start | bytes 884744 | tf_op jit(solution)/shard_map/ppermute | solution.py:120
  333.8 13.7 %collective-permute-start.9 = (bf16[3,1,64,768]{3,2,0,1:T(8,128)(2,1)S(1)}, bf16[3,1,64,768]{3,2,0,1:T(8,128)(2,1)S(1)}, u32[]{:S(2)}, u32[]{:S(2)}) collective-permute-start(bf16[3,1,64,768]{3,2,0,1:T(8,128)(2,1)S(1)} %get-tuple-element.120), channel_id=1, source_target_pairs={{0,1},{1,0},{2,3},{3,2},{4,5},{5,4},{6,7},{7,6},{8,9},{9,8},{10,11... | collective-permute-start | bytes 884744 | tf_op jit(solution)/shard_map/ppermute | solution.py:120
  340.2 206.1 %collective-permute-start.32 = (bf16[2,2,2,2,24,3072]{5,4,0,1,3,2:T(8,128)(2,1)}, bf16[2,2,2,2,24,3072]{5,4,0,1,3,2:T(8,128)(2,1)}, u32[]{:S(2)}, u32[]{:S(2)}) collective-permute-start(bf16[2,2,2,2,24,3072]{5,4,0,1,3,2:T(8,128)(2,1)} %bitcast.331), channel_id=1, source_target_pairs={{0,1},{1,0},{2,3},{3,2},{4,5},{5,4},{6,7},{7,6},{8,9},{9,8},{10,11... | collective-permute-start | bytes 7077896 | tf_op jit(solution)/shard_map/ppermute | solution.py:29
  399.5 20.4 %all-to-all-start.1 = ((bf16[3,4,64,768]{3,2,0,1:T(8,128)(2,1)}), bf16[3,4,64,768]{3,2,0,1:T(8,128)(2,1)}, u32[]{:S(2)}, u32[]{:S(2)}) async-start(bf16[3,4,64,768]{3,2,0,1:T(8,128)(2,1)} %copy.127), calls=%async_computation.1 | async-start | bytes 2359296 | tf_op jit(solution)/shard_map/all_to_all | solution.py:133
  413.1 86.0 %collective-permute-start.22 = (bf16[2,2,2,2,24,1536]{5,4,3,2,1,0:T(8,128)(2,1)}, bf16[2,2,2,2,24,1536]{5,4,3,2,1,0:T(8,128)(2,1)}, u32[]{:S(2)}, u32[]{:S(2)}) collective-permute-start(bf16[2,2,2,2,24,1536]{5,4,3,2,1,0:T(8,128)(2,1)} %dynamic-slice_bitcast_fusion.2), channel_id=1, source_target_pairs={{0,1},{1,0},{2,3},{3,2},{4,5},{5,4},{6,7},{7,6},{8,9},{9,8},{10,11... | collective-permute-start | bytes 3538952 | tf_op jit(solution)/shard_map/ppermute | solution.py:29
  436.8 24.8 %collective-permute-start.12 = (bf16[3,16,1,768]{3,2,1,0:T(2,128)(2,1)}, bf16[3,16,1,768]{3,2,1,0:T(2,128)(2,1)}, u32[]{:S(2)}, u32[]{:S(2)}) collective-permute-start(bf16[3,16,1,768]{3,2,1,0:T(2,128)(2,1)} %broadcast_select_fusion.11), channel_id=1, source_target_pairs={{0,1},{1,0},{2,3},{3,2},{4,5},{5,4},{6,7},{7,6},{8,9},{9,8},{10,11... | collective-permute-start | bytes 221192 | tf_op jit(solution)/shard_map/ppermute | solution.py:29
  465.6 83.3 %collective-permute-start.27 = (bf16[2,2,2,2,24,1664]{5,4,0,1,2,3:T(8,128)(2,1)}, bf16[2,2,2,2,24,1664]{5,4,0,1,2,3:T(8,128)(2,1)}, u32[]{:S(2)}, u32[]{:S(2)}) collective-permute-start(bf16[2,2,2,2,24,1664]{5,4,0,1,2,3:T(8,128)(2,1)} %bitcast.332), channel_id=1, source_target_pairs={{0,1},{1,0},{2,3},{3,2},{4,5},{5,4},{6,7},{7,6},{8,9},{9,8},{10,11... | collective-permute-start | bytes 3833864 | tf_op jit(solution)/shard_map/ppermute | solution.py:29
  486.9 13.8 %collective-permute-start.19 = (f32[1,3,4608]{2,1,0:T(4,128)S(1)}, f32[1,3,4608]{2,1,0:T(4,128)S(1)}, u32[]{:S(2)}, u32[]{:S(2)}) collective-permute-start(f32[1,3,4608]{2,1,0:T(4,128)S(1)} %bitcast.364), channel_id=1, source_target_pairs={{0,4},{4,0},{8,12},{12,8},{16,20},{20,16},{24,28},{28,24},{1,5},{5... | collective-permute-start | bytes 165896 | tf_op jit(solution)/shard_map/ppermute | solution.py:29
  503.4 21.1 %collective-permute-start.23 = (bf16[2,2,2,24,1536]{4,3,2,1,0:T(8,128)(2,1)}, bf16[2,2,2,24,1536]{4,3,2,1,0:T(8,128)(2,1)}, u32[]{:S(2)}, u32[]{:S(2)}) collective-permute-start(bf16[2,2,2,24,1536]{4,3,2,1,0:T(8,128)(2,1)} %dynamic-slice_bitcast_fusion.6), channel_id=1, source_target_pairs={{0,4},{4,0},{8,12},{12,8},{16,20},{20,16},{24,28},{28,24},{1,5},{5... | collective-permute-start | bytes 1769480 | tf_op jit(solution)/shard_map/ppermute | solution.py:29
  506.4 14.9 %collective-permute-start.21 = (f32[4,3,4608]{2,1,0:T(4,128)S(1)}, f32[4,3,4608]{2,1,0:T(4,128)S(1)}, u32[]{:S(2)}, u32[]{:S(2)}) collective-permute-start(f32[4,3,4608]{2,1,0:T(4,128)S(1)} %pad_maximum_fusion.18), channel_id=1, source_target_pairs={{0,16},{4,20},{8,24},{12,28},{16,0},{20,4},{24,8},{28,12},{1,17},{... | collective-permute-start | bytes 663560 | tf_op jit(solution)/shard_map/ppermute | solution.py:29
  511.7 53.4 %collective-permute-start.38 = (bf16[2,2,2,96,768]{4,3,0,1,2:T(8,128)(2,1)}, bf16[2,2,2,96,768]{4,3,0,1,2:T(8,128)(2,1)}, u32[]{:S(2)}, u32[]{:S(2)}) collective-permute-start(bf16[2,2,2,96,768]{4,3,0,1,2:T(8,128)(2,1)} %dynamic-slice_bitcast_fusion), channel_id=1, source_target_pairs={{0,2},{1,3},{2,0},{3,1},{4,6},{5,7},{6,4},{7,5},{8,10},{9,11},{10,... | collective-permute-start | bytes 3538952 | tf_op jit(solution)/shard_map/ppermute | solution.py:29
  525.9 18.6 %collective-permute-start.24 = (bf16[2,2,24,1536]{3,2,1,0:T(8,128)(2,1)S(1)}, bf16[2,2,24,1536]{3,2,1,0:T(8,128)(2,1)S(1)}, u32[]{:S(2)}, u32[]{:S(2)}) collective-permute-start(bf16[2,2,24,1536]{3,2,1,0:T(8,128)(2,1)S(1)} %dynamic-slice_bitcast_fusion.10), channel_id=1, source_target_pairs={{0,2},{1,3},{2,0},{3,1},{4,6},{5,7},{6,4},{7,5},{8,10},{9,11},{10,... | collective-permute-start | bytes 884744 | tf_op jit(solution)/shard_map/ppermute | solution.py:29
  544.6 7.7 %collective-permute-start.25 = (bf16[2,24,1536]{2,1,0:T(8,128)(2,1)S(1)}, bf16[2,24,1536]{2,1,0:T(8,128)(2,1)S(1)}, u32[]{:S(2)}, u32[]{:S(2)}) collective-permute-start(bf16[2,24,1536]{2,1,0:T(8,128)(2,1)S(1)} %dynamic-slice_bitcast_fusion.22), channel_id=1, source_target_pairs={{0,8},{4,12},{8,0},{12,4},{16,24},{20,28},{24,16},{28,20},{1,9},{5... | collective-permute-start | bytes 442376 | tf_op jit(solution)/shard_map/ppermute | solution.py:29
  550.6 13.7 %collective-permute-start.28 = (bf16[2,2,2,24,1664]{4,3,0,1,2:T(8,128)(2,1)S(1)}, bf16[2,2,2,24,1664]{4,3,0,1,2:T(8,128)(2,1)S(1)}, u32[]{:S(2)}, u32[]{:S(2)}) collective-permute-start(bf16[2,2,2,24,1664]{4,3,0,1,2:T(8,128)(2,1)S(1)} %dynamic-slice_bitcast_fusion.3), channel_id=1, source_target_pairs={{0,2},{1,3},{2,0},{3,1},{4,6},{5,7},{6,4},{7,5},{8,10},{9,11},{10,... | collective-permute-start | bytes 1916936 | tf_op jit(solution)/shard_map/ppermute | solution.py:29
  555.1 45.6 %collective-permute-start.33 = (bf16[2,2,2,24,3072]{4,3,0,1,2:T(8,128)(2,1)S(1)}, bf16[2,2,2,24,3072]{4,3,0,1,2:T(8,128)(2,1)S(1)}, u32[]{:S(2)}, u32[]{:S(2)}) collective-permute-start(bf16[2,2,2,24,3072]{4,3,0,1,2:T(8,128)(2,1)S(1)} %dynamic-slice_bitcast_fusion.1), channel_id=1, source_target_pairs={{0,4},{4,0},{8,12},{12,8},{16,20},{20,16},{24,28},{28,24},{1,5},{5... | collective-permute-start | bytes 3538952 | tf_op jit(solution)/shard_map/ppermute | solution.py:29
  564.5 26.4 %collective-permute-start.29 = (bf16[2,2,24,1664]{3,2,0,1:T(8,128)(2,1)S(1)}, bf16[2,2,24,1664]{3,2,0,1:T(8,128)(2,1)S(1)}, u32[]{:S(2)}, u32[]{:S(2)}) collective-permute-start(bf16[2,2,24,1664]{3,2,0,1:T(8,128)(2,1)S(1)} %dynamic-slice_bitcast_fusion.7), channel_id=1, source_target_pairs={{0,4},{4,0},{8,12},{12,8},{16,20},{20,16},{24,28},{28,24},{1,5},{5... | collective-permute-start | bytes 958472 | tf_op jit(solution)/shard_map/ppermute | solution.py:29
  566.8 32.6 %collective-permute-start.39 = (bf16[2,2,96,768]{3,2,0,1:T(8,128)(2,1)S(1)}, bf16[2,2,96,768]{3,2,0,1:T(8,128)(2,1)S(1)}, u32[]{:S(2)}, u32[]{:S(2)}) collective-permute-start(bf16[2,2,96,768]{3,2,0,1:T(8,128)(2,1)S(1)} %dynamic-slice_bitcast_fusion.4), channel_id=1, source_target_pairs={{0,4},{4,0},{8,12},{12,8},{16,20},{20,16},{24,28},{28,24},{1,5},{5... | collective-permute-start | bytes 1769480 | tf_op jit(solution)/shard_map/ppermute | solution.py:29
  591.0 10.2 %collective-permute-start.30 = (bf16[2,24,1664]{2,1,0:T(8,128)(2,1)S(1)}, bf16[2,24,1664]{2,1,0:T(8,128)(2,1)S(1)}, u32[]{:S(2)}, u32[]{:S(2)}) collective-permute-start(bf16[2,24,1664]{2,1,0:T(8,128)(2,1)S(1)} %dynamic-slice_bitcast_fusion.19), channel_id=1, source_target_pairs={{0,8},{4,12},{8,0},{12,4},{16,24},{20,28},{24,16},{28,20},{1,9},{5... | collective-permute-start | bytes 479240 | tf_op jit(solution)/shard_map/ppermute | solution.py:29
  600.3 17.9 %collective-permute-start.40 = (bf16[2,96,768]{2,1,0:T(8,128)(2,1)}, bf16[2,96,768]{2,1,0:T(8,128)(2,1)}, u32[]{:S(2)}, u32[]{:S(2)}) collective-permute-start(bf16[2,96,768]{2,1,0:T(8,128)(2,1)} %dynamic-slice_bitcast_fusion.8), channel_id=1, source_target_pairs={{0,8},{4,12},{8,0},{12,4},{16,24},{20,28},{24,16},{28,20},{1,9},{5... | collective-permute-start | bytes 884744 | tf_op jit(solution)/shard_map/ppermute | solution.py:29
  603.1 12.0 %collective-permute-start.34 = (bf16[2,2,24,3072]{3,2,0,1:T(8,128)(2,1)}, bf16[2,2,24,3072]{3,2,0,1:T(8,128)(2,1)}, u32[]{:S(2)}, u32[]{:S(2)}) collective-permute-start(bf16[2,2,24,3072]{3,2,0,1:T(8,128)(2,1)} %dynamic-slice_bitcast_fusion.5), channel_id=1, source_target_pairs={{0,2},{1,3},{2,0},{3,1},{4,6},{5,7},{6,4},{7,5},{8,10},{9,11},{10,... | collective-permute-start | bytes 1769480 | tf_op jit(solution)/shard_map/ppermute | solution.py:29
  616.5 9.9 %collective-permute-start.35 = (bf16[2,24,3072]{2,1,0:T(8,128)(2,1)S(1)}, bf16[2,24,3072]{2,1,0:T(8,128)(2,1)S(1)}, u32[]{:S(2)}, u32[]{:S(2)}) collective-permute-start(bf16[2,24,3072]{2,1,0:T(8,128)(2,1)S(1)} %dynamic-slice_bitcast_fusion.9), channel_id=1, source_target_pairs={{0,8},{4,12},{8,0},{12,4},{16,24},{20,28},{24,16},{28,20},{1,9},{5... | collective-permute-start | bytes 884744 | tf_op jit(solution)/shard_map/ppermute | solution.py:29
  619.3 8.2 %collective-permute-start.41 = (bf16[96,768]{1,0:T(8,128)(2,1)S(1)}, bf16[96,768]{1,0:T(8,128)(2,1)S(1)}, u32[]{:S(2)}, u32[]{:S(2)}) collective-permute-start(bf16[96,768]{1,0:T(8,128)(2,1)S(1)} %dynamic-slice_bitcast_fusion.20), channel_id=1, source_target_pairs={{0,16},{4,20},{8,24},{12,28},{16,0},{20,4},{24,8},{28,12},{1,17},{... | collective-permute-start | bytes 442376 | tf_op jit(solution)/shard_map/ppermute | solution.py:29
  (156 other events, 1117.0 us)
